TPU v7x, 32 devices: a whole 2x2x4 slice. The times are simulated.
32 devices in a mesh: vox: 16 (over z, x, core), subj: 2 (over y).
Axes of the slice: x: 2, y: 2, z: 4, core: 2. Of those that a mesh axis runs over, the one named last changes fastest.
Arguments:
- series: bfloat16 [8, 4096, 512], P('subj', 'vox'), may hold values from -6 to 6
- live_mask: int32 [4096], P('vox'), may hold values from 0 to 1, as said below
- neighbours: int32 [4096, 13], P('vox'), may hold values from -1 to 510, as said below
- start_vectors: float32 [4096, 64], P('vox'), may hold values from -60 to 60
Outputs:
- embedding: float32 [4096, 64], P('vox')
Inputs may be any that keep to these rules, and one draw needn't show every extreme that they name: `live_mask`: within each aligned block of 128 voxel slots the live slots are a leading run of 1 to 128 slots. `neighbours`: slot n of voxel i names voxel (i // 256 - 1) * 256 + n, which is live and lies before i; the entries of a row are distinct or -1; rows of dead voxels are all -1; rows of the first 256 voxels name no slot under 256.
All inputs are finite; a program needn't handle non-finite values.
Results may differ from a plain program's by a relative error of at most 0.0024.
Values may be sent and summed in bfloat16 or wider, within the bound.
No kernel may reach another device: no remote copies, remote signals or barrier semaphores. Data moves between devices by JAX's collectives and lax.ppermute only.
A program may use at most 64 MiB of HBM per device.

v0:
```python
import math
import jax
import jax.numpy as jnp
from jax import lax
from jax.sharding import PartitionSpec as P

ITERS = 3


def shifted(shard, axis, by):
    count = lax.axis_size(axis)
    pairs = [(i, i + by) for i in range(count) if 0 <= i + by < count]
    return lax.ppermute(shard, axis, pairs)


def as_sent(shard):
    return jax.tree.map(lambda a: a.astype(jnp.bfloat16) if a.dtype == jnp.float32 else a, shard)


def standard(block):
    values = block.astype(jnp.float32)
    center = values - jnp.mean(values, axis=-1, keepdims=True)
    spread = jnp.mean(center * center, axis=-1, keepdims=True)
    return (center * lax.rsqrt(spread + 1e-05)).astype(jnp.bfloat16)


def orthonormal(images):
    gram_matrix = jnp.dot(images.T, images, precision=lax.Precision.HIGHEST)
    gram_matrix = lax.psum(gram_matrix, "vox")
    factor = jnp.linalg.cholesky(gram_matrix)
    return lax.linalg.triangular_solve(
        factor, images, left_side=False, lower=True, transpose_a=True
    )


def dense_graph(weight, slots, columns_total):
    column_ids = jnp.arange(columns_total, dtype=jnp.int32)
    matrix = jnp.zeros((weight.shape[0], columns_total), jnp.float32)
    for offset in range(weight.shape[1]):
        hits = (slots[:, offset][:, None] == column_ids[None, :]).astype(jnp.float32)
        matrix = matrix + weight[:, offset][:, None] * hits
    return matrix


def product(left, right):
    return jnp.dot(left, right, precision=lax.Precision.HIGHEST)


def on_device(series, live_mask, neighbours, start_vectors):
    voxels_here = series.shape[1]
    frames = series.shape[2]
    subjects = series.shape[0] * lax.axis_size("subj")
    scale_factor = 0.5 / math.sqrt(frames * subjects)
    zscored = standard(series)
    earlier = shifted(zscored, "vox", 1)
    window = jnp.concatenate([earlier, zscored], axis=1)
    present = neighbours >= 0
    safe_slots = jnp.maximum(neighbours, 0)
    columns = []
    for offset in range(neighbours.shape[1]):
        picked = jnp.take(window, safe_slots[:, offset], axis=1)
        columns.append(
            jnp.einsum("svf,svf->v", zscored, picked, preferred_element_type=jnp.float32)
        )
    partial_sums = jnp.stack(columns, axis=1)
    summed = lax.psum(partial_sums, "subj")
    weight = jnp.where(present, jnp.exp(scale_factor * summed), 0.0)
    living = live_mask.astype(jnp.float32)
    local_graph = dense_graph(weight, neighbours, 2 * voxels_here)
    owed = jnp.sum(local_graph, axis=0)
    received = shifted(owed[:voxels_here], "vox", -1)
    degree = 1.0 + jnp.sum(weight, axis=1) + owed[voxels_here:] + received
    scaling = living * lax.rsqrt(degree)
    vectors = living[:, None] * start_vectors
    for repeat in range(ITERS):
        scaled = scaling[:, None] * vectors
        earlier_rows = shifted(as_sent(scaled), "vox", 1).astype(scaled.dtype)
        window_rows = jnp.concatenate([earlier_rows, scaled], axis=0)
        forward = product(local_graph, window_rows)
        returns = product(local_graph.T, scaled)
        arrived = shifted(as_sent(returns[:voxels_here]), "vox", -1)
        images = 0.5 * (
            vectors + scaling[:, None] * (scaled + forward + returns[voxels_here:] + arrived)
        )
        vectors = orthonormal(images)
    return vectors


def solution(mesh):
    placed = (P("subj", "vox", None), P("vox"), P("vox", None), P("vox", None))
    return jax.shard_map(
        on_device, mesh=mesh, in_specs=placed, out_specs=P("vox", None), check_vma=False
    )
```

profile of v0, /device:TPU:0, one launch (start us, length us, event | category | flops | bytes accessed | tf_op | source)
XLA Modules:
  0.0 326.5 jit_solution(9285607745963571878)
XLA Ops:
  0.0 2.1 convert_reduce_fusion
  5.0 2.6 collective-permute-start
  11.6 2.5 gather_fusion.3
  14.0 2.5 gather_fusion.2
  16.5 2.5 gather_fusion.1
  19.0 2.4 gather_fusion
  21.5 2.5 gather_fusion.12
  24.0 2.5 gather_fusion.11
  26.5 2.5 gather_fusion.10
  28.9 2.4 gather_fusion.9
  31.4 2.5 gather_fusion.8
  33.9 2.5 gather_fusion.7
  36.4 2.7 gather_fusion.6
  39.1 2.5 gather_fusion.5
  41.5 2.5 gather_fusion.4
  44.1 9.5 %fusion.7 = (f32[256]{0:T(256)S(1)}, f32[256]{0:T(256)S(1)}, f32[256]{0:T(256)S(1)}, f32[256]{0:T(256)S(1)}) fusion(bf16[256,4,512]{2,1,0:T(4,128)(2,1)} %gather_fusion.3, pred[256]{0:T(512)(128)(4,1)S(1)} %get-tuple-element.72, bf16[256,4,512]{2,1,0:T(4,128)(2,1)} %gather_fusion.2, pred[256]{0:T(512)(128)(4,1)S(1)} %get-tuple-element.73, ...), kind=kLoop, calls=%fused_computation.35 | loop fusion | flops 11009024 | bytes 5256192 | tf_op jit(solution)/shard_map/svf,svf->v/dot_general | solution.py:63
  53.7 14.7 %fusion.16 = (f32[256]{0:T(256)S(1)}, f32[256]{0:T(256)S(1)}, f32[256]{0:T(256)S(1)}, f32[256]{0:T(256)S(1)}, f32[256]{0:T(256)S(1)}, /*index=5*/f32[256]{0:T(25...) fusion(bf16[256,4,512]{2,1,0:T(4,128)(2,1)S(1)} %copy-done.1, pred[256]{0:T(512)(128)(4,1)S(1)} %get-tuple-element.76, ...), kind=kLoop, calls=%fused_computation.44 | loop fusion | flops 21493504 | bytes 10505472 | tf_op jit(solution)/shard_map/svf,svf->v/dot_general | solution.py:63
  68.5 9.0 %psum.28 = f32[256,13]{0,1:T(8,128)S(1)} all-reduce(f32[256,13]{0,1:T(8,128)S(1)} %stack.55), channel_id=1, replica_groups=mesh['vox'=16,'subj'=2] {'subj'}, use_global_device_ids=true, to_apply=%region_2.0 | all-reduce | flops 3328 | bytes 26624 | tf_op jit(solution)/shard_map/psum | solution.py:66
  79.8 9.8 %collective-permute-done.1 = f32[256]{0:T(256)S(1)} collective-permute-done((f32[256]{0:T(256)S(1)}, f32[256]{0:T(256)S(1)}, u32[]{:S(2)}, u32[]{:S(2)}) %collective-permute-start.1) | collective-permute-done | bytes 1056 | tf_op jit(solution)/shard_map/ppermute | solution.py:13
  89.6 7.1 %collective-permute-start.2 = (bf16[256,64]{0,1:T(8,128)(2,1)S(1)}, bf16[256,64]{0,1:T(8,128)(2,1)S(1)}, u32[]{:S(2)}, u32[]{:S(2)}) collective-permute-start(bf16[256,64]{0,1:T(8,128)(2,1)S(1)} %get-tuple-element.25), channel_id=1, source_target_pairs={{0,2},{2,4},{4,6},{6,8},{8,10},{10,12},{12,14},{14,16},{16,18},{18... | collective-permute-start | bytes 98312 | tf_op jit(solution)/shard_map/ppermute | solution.py:13
  98.5 1.8 collective-permute-done.3
  101.1 60.4 %psum.29 = f32[64,64]{0,1:T(8,128)S(1)} all-reduce(f32[64,64]{0,1:T(8,128)S(1)} %fusion.66), channel_id=1, replica_groups=mesh['vox'=16,'subj'=2] {'vox'}, use_global_device_ids=true, to_apply=%region_5.7 | all-reduce | flops 4096 | bytes 32768 | tf_op jit(solution)/shard_map/psum | solution.py:29
  161.6 5.8 %cholesky.59 = f32[64,64]{1,0:T(8,128)S(1)} custom-call(f32[64,64]{1,0:T(8,128)S(1)} %fusion.49), custom_call_target="Cholesky" | custom-call | tf_op jit(solution)/shard_map/jit(cholesky)/cholesky | solution.py:30
  168.8 4.9 %custom-call.7 = f32[1,64,64]{1,2,0:T(8,128)S(1)} custom-call(f32[1,64,64]{2,1,0:T(8,128)S(1)} %fusion.41), custom_call_target="InvertDiagBlocksLowerTriangular" | custom-call | tf_op jit(solution)/shard_map/triangular_solve/custom-call.0 | solution.py:31
  177.1 1.8 collective-permute-done.5
  179.7 57.9 %psum.30 = f32[64,64]{0,1:T(8,128)S(1)} all-reduce(f32[64,64]{0,1:T(8,128)S(1)} %fusion.68), channel_id=1, replica_groups=mesh['vox'=16,'subj'=2] {'vox'}, use_global_device_ids=true, to_apply=%region_8.12 | all-reduce | flops 4096 | bytes 32768 | tf_op jit(solution)/shard_map/psum | solution.py:29
  237.6 5.8 %cholesky.70 = f32[64,64]{1,0:T(8,128)S(1)} custom-call(f32[64,64]{1,0:T(8,128)S(1)} %fusion.47), custom_call_target="Cholesky" | custom-call | tf_op jit(solution)/shard_map/jit(cholesky)/cholesky | solution.py:30
  244.8 4.9 %custom-call.8 = f32[1,64,64]{1,2,0:T(8,128)S(1)} custom-call(f32[1,64,64]{2,1,0:T(8,128)S(1)} %fusion.42), custom_call_target="InvertDiagBlocksLowerTriangular" | custom-call | tf_op jit(solution)/shard_map/triangular_solve/custom-call.0 | solution.py:31
  253.1 1.8 collective-permute-done.7
  255.7 57.7 %psum.31 = f32[64,64]{0,1:T(8,128)S(1)} all-reduce(f32[64,64]{0,1:T(8,128)S(1)} %fusion.70), channel_id=1, replica_groups=mesh['vox'=16,'subj'=2] {'vox'}, use_global_device_ids=true, to_apply=%region_9.13 | all-reduce | flops 4096 | bytes 32768 | tf_op jit(solution)/shard_map/psum | solution.py:29
  313.6 5.8 %cholesky.81 = f32[64,64]{1,0:T(8,128)S(1)} custom-call(f32[64,64]{1,0:T(8,128)S(1)} %fusion.45), custom_call_target="Cholesky" | custom-call | tf_op jit(solution)/shard_map/jit(cholesky)/cholesky | solution.py:30
  320.7 4.9 %custom-call.9 = f32[1,64,64]{1,2,0:T(8,128)S(1)} custom-call(f32[1,64,64]{2,1,0:T(8,128)S(1)} %fusion.43), custom_call_target="InvertDiagBlocksLowerTriangular" | custom-call | tf_op jit(solution)/shard_map/triangular_solve/custom-call.0 | solution.py:31
  (124 shorter events, 25.0 us)
Async XLA Ops:
  0.0 2.2 copy-start
  2.1 5.5 %copy-start.7 = (s32[256,13]{0,1:T(8,128)S(1)}, s32[256,13]{0,1:T(8,128)}, u32[]{:S(2)}) copy-start(s32[256,13]{0,1:T(8,128)} %param.11) | copy-start | bytes 39940
  5.0 5.2 %collective-permute-start = (bf16[4,256,512]{2,0,1:T(4,128)(2,1)S(1)}, bf16[4,256,512]{2,0,1:T(4,128)(2,1)S(1)}, u32[]{:S(2)}, u32[]{:S(2)}) collective-permute-start(bf16[4,256,512]{2,0,1:T(4,128)(2,1)S(1)} %fusion.3), channel_id=1, source_target_pairs={{0,2},{2,4},{4,6},{6,8},{8,10},{10,12},{12,14},{14,16},{16,18},{18... | collective-permute-start | bytes 3145736 | tf_op jit(solution)/shard_map/ppermute | solution.py:13
  44.0 9.6 %copy-start.1 = (bf16[256,4,512]{2,1,0:T(4,128)(2,1)S(1)}, bf16[256,4,512]{2,1,0:T(4,128)(2,1)}, u32[]{:S(2)}) copy-start(bf16[256,4,512]{2,1,0:T(4,128)(2,1)} %gather_fusion.12) | copy-start | bytes 3145732
  44.0 9.6 %copy-start.2 = (bf16[256,4,512]{2,1,0:T(4,128)(2,1)S(1)}, bf16[256,4,512]{2,1,0:T(4,128)(2,1)}, u32[]{:S(2)}) copy-start(bf16[256,4,512]{2,1,0:T(4,128)(2,1)} %gather_fusion.11) | copy-start | bytes 3145732
  44.0 9.6 %copy-start.3 = (bf16[256,4,512]{2,1,0:T(4,128)(2,1)S(1)}, bf16[256,4,512]{2,1,0:T(4,128)(2,1)}, u32[]{:S(2)}) copy-start(bf16[256,4,512]{2,1,0:T(4,128)(2,1)} %gather_fusion.10) | copy-start | bytes 3145732
  44.0 9.6 %copy-start.4 = (bf16[256,4,512]{2,1,0:T(4,128)(2,1)S(1)}, bf16[256,4,512]{2,1,0:T(4,128)(2,1)}, u32[]{:S(2)}) copy-start(bf16[256,4,512]{2,1,0:T(4,128)(2,1)} %gather_fusion.9) | copy-start | bytes 3145732
  44.0 9.6 %copy-start.5 = (bf16[256,4,512]{2,1,0:T(4,128)(2,1)S(1)}, bf16[256,4,512]{2,1,0:T(4,128)(2,1)}, u32[]{:S(2)}) copy-start(bf16[256,4,512]{2,1,0:T(4,128)(2,1)} %gather_fusion.8) | copy-start | bytes 3145732
  44.0 9.6 %copy-start.9 = (pred[256]{0:T(512)(128)(4,1)S(1)}, pred[256]{0:T(512)(128)(4,1)}, u32[]{:S(2)}) copy-start(pred[256]{0:T(512)(128)(4,1)} %get-tuple-element.78) | copy-start | bytes 772
  44.0 9.6 %copy-start.10 = (pred[256]{0:T(512)(128)(4,1)S(1)}, pred[256]{0:T(512)(128)(4,1)}, u32[]{:S(2)}) copy-start(pred[256]{0:T(512)(128)(4,1)} %get-tuple-element.79) | copy-start | bytes 772
  44.0 9.6 %copy-start.11 = (pred[256]{0:T(512)(128)(4,1)S(1)}, pred[256]{0:T(512)(128)(4,1)}, u32[]{:S(2)}) copy-start(pred[256]{0:T(512)(128)(4,1)} %get-tuple-element.80) | copy-start | bytes 772
  44.1 9.6 %copy-start.12 = (pred[256]{0:T(512)(128)(4,1)S(1)}, pred[256]{0:T(512)(128)(4,1)}, u32[]{:S(2)}) copy-start(pred[256]{0:T(512)(128)(4,1)} %get-tuple-element.81) | copy-start | bytes 772
  44.1 9.6 %copy-start.13 = (pred[256]{0:T(512)(128)(4,1)S(1)}, pred[256]{0:T(512)(128)(4,1)}, u32[]{:S(2)}) copy-start(pred[256]{0:T(512)(128)(4,1)} %get-tuple-element.82) | copy-start | bytes 772
  44.1 9.6 %copy-start.14 = (pred[256]{0:T(512)(128)(4,1)S(1)}, pred[256]{0:T(512)(128)(4,1)}, u32[]{:S(2)}) copy-start(pred[256]{0:T(512)(128)(4,1)} %get-tuple-element.83) | copy-start | bytes 772
  44.1 9.6 %copy-start.15 = (pred[256]{0:T(512)(128)(4,1)S(1)}, pred[256]{0:T(512)(128)(4,1)}, u32[]{:S(2)}) copy-start(pred[256]{0:T(512)(128)(4,1)} %compare_and_fusion.8) | copy-start | bytes 772
  53.7 26.1 %copy-start.8 = (s32[256]{0:T(256)S(1)}, s32[256]{0:T(256)}, u32[]{:S(2)}) copy-start(s32[256]{0:T(256)} %param.10) | copy-start | bytes 3076
  53.7 35.9 %copy-start.6 = (f32[256,64]{0,1:T(8,128)S(1)}, f32[256,64]{0,1:T(8,128)}, u32[]{:S(2)}) copy-start(f32[256,64]{0,1:T(8,128)} %param.12) | copy-start | bytes 196612
  78.5 11.1 %collective-permute-start.1 = (f32[256]{0:T(256)S(1)}, f32[256]{0:T(256)S(1)}, u32[]{:S(2)}, u32[]{:S(2)}) collective-permute-start(f32[256]{0:T(256)S(1)} %slice.190), channel_id=1, source_target_pairs={{2,0},{4,2},{6,4},{8,6},{10,8},{12,10},{14,12},{16,14},{18,16},{20... | collective-permute-start | bytes 3080 | tf_op jit(solution)/shard_map/ppermute | solution.py:13
  89.6 8.8 %collective-permute-start.2 = (bf16[256,64]{0,1:T(8,128)(2,1)S(1)}, bf16[256,64]{0,1:T(8,128)(2,1)S(1)}, u32[]{:S(2)}, u32[]{:S(2)}) collective-permute-start(bf16[256,64]{0,1:T(8,128)(2,1)S(1)} %get-tuple-element.25), channel_id=1, source_target_pairs={{0,2},{2,4},{4,6},{6,8},{8,10},{10,12},{12,14},{14,16},{16,18},{18... | collective-permute-start | bytes 98312 | tf_op jit(solution)/shard_map/ppermute | solution.py:13
  97.1 3.1 collective-permute-start.3
  174.0 3.1 collective-permute-start.4
  175.7 3.1 collective-permute-start.5
  250.0 3.1 collective-permute-start.6
  251.8 3.1 collective-permute-start.7
where the time goes:
time: 327 us
  blocking collectives  185 us (57%)
  other arithmetic  70 us (21%)
  local copies, waits for them, and re-layouts  32.8 us (10%)
  starting transfers between devices  17.5 us (5%)
  waiting for transfers between devices  15.1 us (5%)
  matrix products  5.26 us (2%)
    psum x3, blocking collectives, orthonormal(): gram_matrix = lax.psum(gram_matrix, 'vox')  176 us
    gather x13, local copies, waits for them, and re-layouts, on_device(): picked = jnp.take(window, safe_slots[:, offset], axis=1)  32.4 us
    dot_general x2, other arithmetic, on_device(): jnp.einsum('svf,svf->v', zscored, picked, preferred_element_type=jnp.floa...  24.1 us
    another operation x9, other arithmetic, orthonormal(): factor = jnp.linalg.cholesky(gram_matrix)  19.6 us
    ppermute x8, starting transfers between devices, shifted(): return lax.ppermute(shard, axis, pairs)  17.5 us
    another operation x6, other arithmetic, orthonormal(): lax.linalg.triangular_solve(factor, images, left_side=False, lower=True,...  16.6 us
    ppermute x8, waiting for transfers between devices, shifted(): return lax.ppermute(shard, axis, pairs)  15.1 us
    psum x1, blocking collectives, on_device(): summed = lax.psum(partial_sums, 'subj')  8.99 us
  transfers between devices with their start and end apart: 8, of which 4 were waited for; matrix products, arithmetic and copies ran while one was open for 1% of the time, Pallas kernels for 0%

commit v1 on v0

--- a/solution.py
+++ b/solution.py
@@ -26,7 +26,11 @@
 
 def orthonormal(images):
     gram_matrix = jnp.dot(images.T, images, precision=lax.Precision.HIGHEST)
-    gram_matrix = lax.psum(gram_matrix, "vox")
+    gram_matrix = gram_matrix
+    for hop in (1, 2, 4, 8):
+        gram_matrix = gram_matrix + lax.ppermute(
+            gram_matrix, "vox", [(dev, dev ^ hop) for dev in range(16)]
+        )
     factor = jnp.linalg.cholesky(gram_matrix)
     return lax.linalg.triangular_solve(
         factor, images, left_side=False, lower=True, transpose_a=True

time: 327 us -> 205 us (0.63)
  blocking collectives: 185 us -> 8.99 us
  starting transfers between devices: 17.5 us -> 44.7 us
  waiting for transfers between devices: 15.1 us -> 41.8 us
    psum x3 -> x0, blocking collectives: 176 us -> none  [orthonormal(): gram_matrix = lax.psum(gram_matrix, 'vox')]
    ppermute x0 -> x12, starting transfers between devices: none -> 27 us  [orthonormal(): lax.ppermute(gram_matrix, 'vox', [(dev, dev ^ hop) for dev in range(16)])]
    ppermute x0 -> x12, waiting for transfers between devices: none -> 22.4 us  [orthonormal(): lax.ppermute(gram_matrix, 'vox', [(dev, dev ^ hop) for dev in range(16)])]
    ppermute x8, waiting for transfers between devices: 15.1 us -> 19.4 us  [shifted(): return lax.ppermute(shard, axis, pairs)]
  transfers between devices with their start and end apart: 8 -> 20, of which waited for: 4 -> 16; matrix products, arithmetic and copies ran while one was open for 1% -> 2% of each run, Pallas kernels for 0% -> 0%
where the time goes in v1:
time: 205 us; the launch traced here: 204 us
  other arithmetic  70.1 us (34%)
  starting transfers between devices  44.7 us (22%)
  waiting for transfers between devices  41.8 us (20%)
  local copies, waits for them, and re-layouts  32.8 us (16%)
  blocking collectives  8.99 us (4%)
  matrix products  5.27 us (3%)
    gather x13, local copies, waits for them, and re-layouts, on_device(): picked = jnp.take(window, safe_slots[:, offset], axis=1)  32.4 us
    ppermute x12, starting transfers between devices, orthonormal(): lax.ppermute(gram_matrix, 'vox', [(dev, dev ^ hop) for dev in range(16)])  27 us
    dot_general x2, other arithmetic, on_device(): jnp.einsum('svf,svf->v', zscored, picked, preferred_element_type=jnp.floa...  24.1 us
    ppermute x12, waiting for transfers between devices, orthonormal(): lax.ppermute(gram_matrix, 'vox', [(dev, dev ^ hop) for dev in range(16)])  22.4 us
    another operation x9, other arithmetic, orthonormal(): factor = jnp.linalg.cholesky(gram_matrix)  19.6 us
    ppermute x8, waiting for transfers between devices, shifted(): return lax.ppermute(shard, axis, pairs)  19.4 us
    ppermute x8, starting transfers between devices, shifted(): return lax.ppermute(shard, axis, pairs)  17.7 us
    another operation x6, other arithmetic, orthonormal(): lax.linalg.triangular_solve(factor, images, left_side=False, lower=True,...  16.6 us
  transfers between devices with their start and end apart: 20, of which 16 were waited for; matrix products, arithmetic and copies ran while one was open for 2% of the time, Pallas kernels for 0%

profile of v1, /device:TPU:0, one launch (start us, length us, event | category | flops | bytes accessed | tf_op | source)
XLA Modules:
  0.0 204.5 jit_solution(17120000626724618931)
XLA Ops:
  5.0 2.6 %collective-permute-start = (bf16[4,256,512]{2,0,1:T(4,128)(2,1)S(1)}, bf16[4,256,512]{2,0,1:T(4,128)(2,1)S(1)}, u32[]{:S(2)}, u32[]{:S(2)}) collective-permute-start(bf16[4,256,512]{2,0,1:T(4,128)(2,1)S(1)} %fusion.3), channel_id=1, source_target_pairs={{0,2},{2,4},{4,6},{6,8},{8,10},{10,12},{12,14},{14,16},{16,18},{18... | collective-permute-start | bytes 3145736 | tf_op jit(solution)/shard_map/ppermute | solution.py:13
  11.6 2.5 %gather_fusion.3 = bf16[256,4,512]{2,1,0:T(4,128)(2,1)} fusion(bf16[4,512,512]{2,0,1:T(4,128)(2,1)S(1)} %pad_maximum_fusion, s32[1024]{0:T(1024)S(1)} %pad_clamp_fusion.9), kind=kCustom, calls=%fused_computation.3.clone | custom fusion | bytes 2098176 | tf_op jit(solution)/shard_map/jit(_take)/gather | solution.py:65
  14.0 2.5 %gather_fusion.2 = bf16[256,4,512]{2,1,0:T(4,128)(2,1)} fusion(bf16[4,512,512]{2,0,1:T(4,128)(2,1)S(1)} %pad_maximum_fusion, s32[1024]{0:T(1024)S(1)} %pad_clamp_fusion.10), kind=kCustom, calls=%fused_computation.2.clone | custom fusion | bytes 2098176 | tf_op jit(solution)/shard_map/jit(_take)/gather | solution.py:65
  16.5 2.5 %gather_fusion.1 = bf16[256,4,512]{2,1,0:T(4,128)(2,1)} fusion(bf16[4,512,512]{2,0,1:T(4,128)(2,1)S(1)} %pad_maximum_fusion, s32[1024]{0:T(1024)S(1)} %pad_clamp_fusion.11), kind=kCustom, calls=%fused_computation.1.clone | custom fusion | bytes 2098176 | tf_op jit(solution)/shard_map/jit(_take)/gather | solution.py:65
  21.5 2.5 %gather_fusion.12 = bf16[256,4,512]{2,1,0:T(4,128)(2,1)} fusion(bf16[4,512,512]{2,0,1:T(4,128)(2,1)S(1)} %pad_maximum_fusion, s32[1024]{0:T(1024)S(1)} %pad_clamp_fusion), kind=kCustom, calls=%fused_computation.12.clone | custom fusion | bytes 2098176 | tf_op jit(solution)/shard_map/jit(_take)/gather | solution.py:65
  24.0 2.5 %gather_fusion.11 = bf16[256,4,512]{2,1,0:T(4,128)(2,1)} fusion(bf16[4,512,512]{2,0,1:T(4,128)(2,1)S(1)} %pad_maximum_fusion, s32[1024]{0:T(1024)S(1)} %pad_clamp_fusion.1), kind=kCustom, calls=%fused_computation.11.clone | custom fusion | bytes 2098176 | tf_op jit(solution)/shard_map/jit(_take)/gather | solution.py:65
  26.5 2.5 %gather_fusion.10 = bf16[256,4,512]{2,1,0:T(4,128)(2,1)} fusion(bf16[4,512,512]{2,0,1:T(4,128)(2,1)S(1)} %pad_maximum_fusion, s32[1024]{0:T(1024)S(1)} %pad_clamp_fusion.2), kind=kCustom, calls=%fused_computation.10.clone | custom fusion | bytes 2098176 | tf_op jit(solution)/shard_map/jit(_take)/gather | solution.py:65
  31.4 2.5 %gather_fusion.8 = bf16[256,4,512]{2,1,0:T(4,128)(2,1)} fusion(bf16[4,512,512]{2,0,1:T(4,128)(2,1)S(1)} %pad_maximum_fusion, s32[1024]{0:T(1024)S(1)} %pad_clamp_fusion.4), kind=kCustom, calls=%fused_computation.8.clone | custom fusion | bytes 2098176 | tf_op jit(solution)/shard_map/jit(_take)/gather | solution.py:65
  33.9 2.5 %gather_fusion.7 = bf16[256,4,512]{2,1,0:T(4,128)(2,1)} fusion(bf16[4,512,512]{2,0,1:T(4,128)(2,1)S(1)} %pad_maximum_fusion, s32[1024]{0:T(1024)S(1)} %pad_clamp_fusion.5), kind=kCustom, calls=%fused_computation.7.clone | custom fusion | bytes 2098176 | tf_op jit(solution)/shard_map/jit(_take)/gather | solution.py:65
  36.4 2.7 %gather_fusion.6 = bf16[256,4,512]{2,1,0:T(4,128)(2,1)} fusion(bf16[4,512,512]{2,0,1:T(4,128)(2,1)S(1)} %pad_maximum_fusion, s32[1024]{0:T(1024)S(1)} %pad_clamp_fusion.6), kind=kCustom, calls=%fused_computation.6.clone | custom fusion | bytes 2098176 | tf_op jit(solution)/shard_map/jit(_take)/gather | solution.py:65
  39.1 2.5 %gather_fusion.5 = bf16[256,4,512]{2,1,0:T(4,128)(2,1)} fusion(bf16[4,512,512]{2,0,1:T(4,128)(2,1)S(1)} %pad_maximum_fusion, s32[1024]{0:T(1024)S(1)} %pad_clamp_fusion.7), kind=kCustom, calls=%fused_computation.5.clone | custom fusion | bytes 2098176 | tf_op jit(solution)/shard_map/jit(_take)/gather | solution.py:65
  41.5 2.5 %gather_fusion.4 = bf16[256,4,512]{2,1,0:T(4,128)(2,1)} fusion(bf16[4,512,512]{2,0,1:T(4,128)(2,1)S(1)} %pad_maximum_fusion, s32[1024]{0:T(1024)S(1)} %pad_clamp_fusion.8), kind=kCustom, calls=%fused_computation.4.clone | custom fusion | bytes 2098176 | tf_op jit(solution)/shard_map/jit(_take)/gather | solution.py:65
  44.1 9.5 %fusion.7 = (f32[256]{0:T(256)S(1)}, f32[256]{0:T(256)S(1)}, f32[256]{0:T(256)S(1)}, f32[256]{0:T(256)S(1)}) fusion(bf16[256,4,512]{2,1,0:T(4,128)(2,1)} %gather_fusion.3, pred[256]{0:T(512)(128)(4,1)S(1)} %get-tuple-element.72, bf16[256,4,512]{2,1,0:T(4,128)(2,1)} %gather_fusion.2, pred[256]{0:T(512)(128)(4,1)S(1)} %get-tuple-element.73, ...), kind=kLoop, calls=%fused_computation.35 | loop fusion | flops 11009024 | bytes 5256192 | tf_op jit(solution)/shard_map/svf,svf->v/dot_general | solution.py:67
  53.7 14.7 %fusion.16 = (f32[256]{0:T(256)S(1)}, f32[256]{0:T(256)S(1)}, f32[256]{0:T(256)S(1)}, f32[256]{0:T(256)S(1)}, f32[256]{0:T(256)S(1)}, /*index=5*/f32[256]{0:T(25...) fusion(bf16[256,4,512]{2,1,0:T(4,128)(2,1)S(1)} %copy-done.1, pred[256]{0:T(512)(128)(4,1)S(1)} %get-tuple-element.76, ...), kind=kLoop, calls=%fused_computation.44 | loop fusion | flops 21493504 | bytes 10505472 | tf_op jit(solution)/shard_map/svf,svf->v/dot_general | solution.py:67
  68.5 9.0 %psum.7 = f32[256,13]{0,1:T(8,128)S(1)} all-reduce(f32[256,13]{0,1:T(8,128)S(1)} %stack.55), channel_id=1, replica_groups=mesh['vox'=16,'subj'=2] {'subj'}, use_global_device_ids=true, to_apply=%region_2.0 | all-reduce | flops 3328 | bytes 26624 | tf_op jit(solution)/shard_map/psum | solution.py:70
  79.8 9.8 %collective-permute-done.1 = f32[256]{0:T(256)S(1)} collective-permute-done((f32[256]{0:T(256)S(1)}, f32[256]{0:T(256)S(1)}, u32[]{:S(2)}, u32[]{:S(2)}) %collective-permute-start.1) | collective-permute-done | bytes 1056 | tf_op jit(solution)/shard_map/ppermute | solution.py:13
  89.6 7.1 %collective-permute-start.2 = (bf16[256,64]{0,1:T(8,128)(2,1)S(1)}, bf16[256,64]{0,1:T(8,128)(2,1)S(1)}, u32[]{:S(2)}, u32[]{:S(2)}) collective-permute-start(bf16[256,64]{0,1:T(8,128)(2,1)S(1)} %get-tuple-element.25), channel_id=1, source_target_pairs={{0,2},{2,4},{4,6},{6,8},{8,10},{10,12},{12,14},{14,16},{16,18},{18... | collective-permute-start | bytes 98312 | tf_op jit(solution)/shard_map/ppermute | solution.py:13
  101.1 2.9 %collective-permute-start.4 = (f32[64,64]{0,1:T(8,128)S(1)}, f32[64,64]{0,1:T(8,128)S(1)}, u32[]{:S(2)}, u32[]{:S(2)}) collective-permute-start(f32[64,64]{0,1:T(8,128)S(1)} %fusion.66), channel_id=1, source_target_pairs={{0,2},{2,0},{4,6},{6,4},{8,10},{10,8},{12,14},{14,12},{16,18},{18,... | collective-permute-start | bytes 49160 | tf_op jit(solution)/shard_map/ppermute | solution.py:31
  104.9 2.6 %collective-permute-start.5 = (f32[64,64]{0,1:T(8,128)S(1)}, f32[64,64]{0,1:T(8,128)S(1)}, u32[]{:S(2)}, u32[]{:S(2)}) collective-permute-start(f32[64,64]{0,1:T(8,128)S(1)} %add.169), channel_id=1, source_target_pairs={{0,4},{2,6},{4,0},{6,2},{8,12},{10,14},{12,8},{14,10},{16,20},{18,... | collective-permute-start | bytes 49160 | tf_op jit(solution)/shard_map/ppermute | solution.py:31
  113.3 2.7 %collective-permute-start.7 = (f32[64,64]{0,1:T(8,128)S(1)}, f32[64,64]{0,1:T(8,128)S(1)}, u32[]{:S(2)}, u32[]{:S(2)}) collective-permute-start(f32[64,64]{0,1:T(8,128)S(1)} %add.171), channel_id=1, source_target_pairs={{0,16},{2,18},{4,20},{6,22},{8,24},{10,26},{12,28},{14,30},{16,0},... | collective-permute-start | bytes 49160 | tf_op jit(solution)/shard_map/ppermute | solution.py:31
  118.2 5.8 %cholesky.59 = f32[64,64]{1,0:T(8,128)S(1)} custom-call(f32[64,64]{1,0:T(8,128)S(1)} %fusion.49), custom_call_target="Cholesky" | custom-call | tf_op jit(solution)/shard_map/jit(cholesky)/cholesky | solution.py:34
  125.4 4.9 %custom-call.7 = f32[1,64,64]{1,2,0:T(8,128)S(1)} custom-call(f32[1,64,64]{2,1,0:T(8,128)S(1)} %fusion.41), custom_call_target="InvertDiagBlocksLowerTriangular" | custom-call | tf_op jit(solution)/shard_map/triangular_solve/custom-call.0 | solution.py:35
  133.9 3.8 %collective-permute-done.9 = bf16[256,64]{0,1:T(8,128)(2,1)S(1)} collective-permute-done((bf16[256,64]{0,1:T(8,128)(2,1)S(1)}, bf16[256,64]{0,1:T(8,128)(2,1)S(1)}, u32[]{:S(2)}, u32[]{:S(2)}) %collective-permute-start.9) | collective-permute-done | bytes 32800 | tf_op jit(solution)/shard_map/ppermute | solution.py:13
  138.5 2.7 %collective-permute-start.10 = (f32[64,64]{0,1:T(8,128)S(1)}, f32[64,64]{0,1:T(8,128)S(1)}, u32[]{:S(2)}, u32[]{:S(2)}) collective-permute-start(f32[64,64]{0,1:T(8,128)S(1)} %fusion.68), channel_id=1, source_target_pairs={{0,2},{2,0},{4,6},{6,4},{8,10},{10,8},{12,14},{14,12},{16,18},{18,... | collective-permute-start | bytes 49160 | tf_op jit(solution)/shard_map/ppermute | solution.py:31
  149.9 2.7 %collective-permute-start.13 = (f32[64,64]{0,1:T(8,128)S(1)}, f32[64,64]{0,1:T(8,128)S(1)}, u32[]{:S(2)}, u32[]{:S(2)}) collective-permute-start(f32[64,64]{0,1:T(8,128)S(1)} %add.179), channel_id=1, source_target_pairs={{0,16},{2,18},{4,20},{6,22},{8,24},{10,26},{12,28},{14,30},{16,0},... | collective-permute-start | bytes 49160 | tf_op jit(solution)/shard_map/ppermute | solution.py:31
  154.9 5.8 %cholesky.70 = f32[64,64]{1,0:T(8,128)S(1)} custom-call(f32[64,64]{1,0:T(8,128)S(1)} %fusion.47), custom_call_target="Cholesky" | custom-call | tf_op jit(solution)/shard_map/jit(cholesky)/cholesky | solution.py:34
  162.0 4.9 %custom-call.8 = f32[1,64,64]{1,2,0:T(8,128)S(1)} custom-call(f32[1,64,64]{2,1,0:T(8,128)S(1)} %fusion.42), custom_call_target="InvertDiagBlocksLowerTriangular" | custom-call | tf_op jit(solution)/shard_map/triangular_solve/custom-call.0 | solution.py:35
  170.3 4.0 %collective-permute-done.15 = bf16[256,64]{0,1:T(8,128)(2,1)S(1)} collective-permute-done((bf16[256,64]{0,1:T(8,128)(2,1)S(1)}, bf16[256,64]{0,1:T(8,128)(2,1)S(1)}, u32[]{:S(2)}, u32[]{:S(2)}) %collective-permute-start.15) | collective-permute-done | bytes 32800 | tf_op jit(solution)/shard_map/ppermute | solution.py:13
  175.2 2.7 %collective-permute-start.16 = (f32[64,64]{0,1:T(8,128)S(1)}, f32[64,64]{0,1:T(8,128)S(1)}, u32[]{:S(2)}, u32[]{:S(2)}) collective-permute-start(f32[64,64]{0,1:T(8,128)S(1)} %fusion.70), channel_id=1, source_target_pairs={{0,2},{2,0},{4,6},{6,4},{8,10},{10,8},{12,14},{14,12},{16,18},{18,... | collective-permute-start | bytes 49160 | tf_op jit(solution)/shard_map/ppermute | solution.py:31
  188.4 3.0 %collective-permute-done.19 = f32[64,64]{0,1:T(8,128)S(1)} collective-permute-done((f32[64,64]{0,1:T(8,128)S(1)}, f32[64,64]{0,1:T(8,128)S(1)}, u32[]{:S(2)}, u32[]{:S(2)}) %collective-permute-start.19) | collective-permute-done | bytes 16416 | tf_op jit(solution)/shard_map/ppermute | solution.py:31
  191.5 5.8 %cholesky.81 = f32[64,64]{1,0:T(8,128)S(1)} custom-call(f32[64,64]{1,0:T(8,128)S(1)} %fusion.45), custom_call_target="Cholesky" | custom-call | tf_op jit(solution)/shard_map/jit(cholesky)/cholesky | solution.py:34
  198.7 4.9 %custom-call.9 = f32[1,64,64]{1,2,0:T(8,128)S(1)} custom-call(f32[1,64,64]{2,1,0:T(8,128)S(1)} %fusion.43), custom_call_target="InvertDiagBlocksLowerTriangular" | custom-call | tf_op jit(solution)/shard_map/triangular_solve/custom-call.0 | solution.py:35
  (157 shorter events, 64.2 us)
Async XLA Ops:
  5.0 5.2 %collective-permute-start = (bf16[4,256,512]{2,0,1:T(4,128)(2,1)S(1)}, bf16[4,256,512]{2,0,1:T(4,128)(2,1)S(1)}, u32[]{:S(2)}, u32[]{:S(2)}) collective-permute-start(bf16[4,256,512]{2,0,1:T(4,128)(2,1)S(1)} %fusion.3), channel_id=1, source_target_pairs={{0,2},{2,4},{4,6},{6,8},{8,10},{10,12},{12,14},{14,16},{16,18},{18... | collective-permute-start | bytes 3145736 | tf_op jit(solution)/shard_map/ppermute | solution.py:13
  44.0 9.6 %copy-start.3 = (bf16[256,4,512]{2,1,0:T(4,128)(2,1)S(1)}, bf16[256,4,512]{2,1,0:T(4,128)(2,1)}, u32[]{:S(2)}) copy-start(bf16[256,4,512]{2,1,0:T(4,128)(2,1)} %gather_fusion.10) | copy-start | bytes 3145732
  44.0 9.6 %copy-start.4 = (bf16[256,4,512]{2,1,0:T(4,128)(2,1)S(1)}, bf16[256,4,512]{2,1,0:T(4,128)(2,1)}, u32[]{:S(2)}) copy-start(bf16[256,4,512]{2,1,0:T(4,128)(2,1)} %gather_fusion.9) | copy-start | bytes 3145732
  44.0 9.6 %copy-start.5 = (bf16[256,4,512]{2,1,0:T(4,128)(2,1)S(1)}, bf16[256,4,512]{2,1,0:T(4,128)(2,1)}, u32[]{:S(2)}) copy-start(bf16[256,4,512]{2,1,0:T(4,128)(2,1)} %gather_fusion.8) | copy-start | bytes 3145732
  44.0 9.6 %copy-start.9 = (pred[256]{0:T(512)(128)(4,1)S(1)}, pred[256]{0:T(512)(128)(4,1)}, u32[]{:S(2)}) copy-start(pred[256]{0:T(512)(128)(4,1)} %get-tuple-element.78) | copy-start | bytes 772
  44.0 9.6 %copy-start.10 = (pred[256]{0:T(512)(128)(4,1)S(1)}, pred[256]{0:T(512)(128)(4,1)}, u32[]{:S(2)}) copy-start(pred[256]{0:T(512)(128)(4,1)} %get-tuple-element.79) | copy-start | bytes 772
  44.0 9.6 %copy-start.11 = (pred[256]{0:T(512)(128)(4,1)S(1)}, pred[256]{0:T(512)(128)(4,1)}, u32[]{:S(2)}) copy-start(pred[256]{0:T(512)(128)(4,1)} %get-tuple-element.80) | copy-start | bytes 772
  44.1 9.6 %copy-start.12 = (pred[256]{0:T(512)(128)(4,1)S(1)}, pred[256]{0:T(512)(128)(4,1)}, u32[]{:S(2)}) copy-start(pred[256]{0:T(512)(128)(4,1)} %get-tuple-element.81) | copy-start | bytes 772
  44.1 9.6 %copy-start.13 = (pred[256]{0:T(512)(128)(4,1)S(1)}, pred[256]{0:T(512)(128)(4,1)}, u32[]{:S(2)}) copy-start(pred[256]{0:T(512)(128)(4,1)} %get-tuple-element.82) | copy-start | bytes 772
  44.1 9.6 %copy-start.14 = (pred[256]{0:T(512)(128)(4,1)S(1)}, pred[256]{0:T(512)(128)(4,1)}, u32[]{:S(2)}) copy-start(pred[256]{0:T(512)(128)(4,1)} %get-tuple-element.83) | copy-start | bytes 772
  44.1 9.6 %copy-start.15 = (pred[256]{0:T(512)(128)(4,1)S(1)}, pred[256]{0:T(512)(128)(4,1)}, u32[]{:S(2)}) copy-start(pred[256]{0:T(512)(128)(4,1)} %compare_and_fusion.8) | copy-start | bytes 772
  53.7 26.1 %copy-start.8 = (s32[256]{0:T(256)S(1)}, s32[256]{0:T(256)}, u32[]{:S(2)}) copy-start(s32[256]{0:T(256)} %param.10) | copy-start | bytes 3076
  53.7 35.9 %copy-start.6 = (f32[256,64]{0,1:T(8,128)S(1)}, f32[256,64]{0,1:T(8,128)}, u32[]{:S(2)}) copy-start(f32[256,64]{0,1:T(8,128)} %param.12) | copy-start | bytes 196612
  78.5 11.1 %collective-permute-start.1 = (f32[256]{0:T(256)S(1)}, f32[256]{0:T(256)S(1)}, u32[]{:S(2)}, u32[]{:S(2)}) collective-permute-start(f32[256]{0:T(256)S(1)} %slice.190), channel_id=1, source_target_pairs={{2,0},{4,2},{6,4},{8,6},{10,8},{12,10},{14,12},{16,14},{18,16},{20... | collective-permute-start | bytes 3080 | tf_op jit(solution)/shard_map/ppermute | solution.py:13
  89.6 8.8 %collective-permute-start.2 = (bf16[256,64]{0,1:T(8,128)(2,1)S(1)}, bf16[256,64]{0,1:T(8,128)(2,1)S(1)}, u32[]{:S(2)}, u32[]{:S(2)}) collective-permute-start(bf16[256,64]{0,1:T(8,128)(2,1)S(1)} %get-tuple-element.25), channel_id=1, source_target_pairs={{0,2},{2,4},{4,6},{6,8},{8,10},{10,12},{12,14},{14,16},{16,18},{18... | collective-permute-start | bytes 98312 | tf_op jit(solution)/shard_map/ppermute | solution.py:13
  97.1 3.1 %collective-permute-start.3 = (bf16[256,64]{0,1:T(8,128)(2,1)S(1)}, bf16[256,64]{0,1:T(8,128)(2,1)S(1)}, u32[]{:S(2)}, u32[]{:S(2)}) collective-permute-start(bf16[256,64]{0,1:T(8,128)(2,1)S(1)} %slice.264), channel_id=1, source_target_pairs={{2,0},{4,2},{6,4},{8,6},{10,8},{12,10},{14,12},{16,14},{18,16},{20... | collective-permute-start | bytes 98312 | tf_op jit(solution)/shard_map/ppermute | solution.py:13
  101.1 3.8 %collective-permute-start.4 = (f32[64,64]{0,1:T(8,128)S(1)}, f32[64,64]{0,1:T(8,128)S(1)}, u32[]{:S(2)}, u32[]{:S(2)}) collective-permute-start(f32[64,64]{0,1:T(8,128)S(1)} %fusion.66), channel_id=1, source_target_pairs={{0,2},{2,0},{4,6},{6,4},{8,10},{10,8},{12,14},{14,12},{16,18},{18,... | collective-permute-start | bytes 49160 | tf_op jit(solution)/shard_map/ppermute | solution.py:31
  104.9 4.5 %collective-permute-start.5 = (f32[64,64]{0,1:T(8,128)S(1)}, f32[64,64]{0,1:T(8,128)S(1)}, u32[]{:S(2)}, u32[]{:S(2)}) collective-permute-start(f32[64,64]{0,1:T(8,128)S(1)} %add.169), channel_id=1, source_target_pairs={{0,4},{2,6},{4,0},{6,2},{8,12},{10,14},{12,8},{14,10},{16,20},{18,... | collective-permute-start | bytes 49160 | tf_op jit(solution)/shard_map/ppermute | solution.py:31
  109.4 3.9 %collective-permute-start.6 = (f32[64,64]{0,1:T(8,128)S(1)}, f32[64,64]{0,1:T(8,128)S(1)}, u32[]{:S(2)}, u32[]{:S(2)}) collective-permute-start(f32[64,64]{0,1:T(8,128)S(1)} %add.170), channel_id=1, source_target_pairs={{0,8},{2,10},{4,12},{6,14},{8,0},{10,2},{12,4},{14,6},{16,24},{18,... | collective-permute-start | bytes 49160 | tf_op jit(solution)/shard_map/ppermute | solution.py:31
  113.3 4.8 %collective-permute-start.7 = (f32[64,64]{0,1:T(8,128)S(1)}, f32[64,64]{0,1:T(8,128)S(1)}, u32[]{:S(2)}, u32[]{:S(2)}) collective-permute-start(f32[64,64]{0,1:T(8,128)S(1)} %add.171), channel_id=1, source_target_pairs={{0,16},{2,18},{4,20},{6,22},{8,24},{10,26},{12,28},{14,30},{16,0},... | collective-permute-start | bytes 49160 | tf_op jit(solution)/shard_map/ppermute | solution.py:31
  130.6 3.3 %collective-permute-start.8 = (bf16[256,64]{0,1:T(8,128)(2,1)S(1)}, bf16[256,64]{0,1:T(8,128)(2,1)S(1)}, u32[]{:S(2)}, u32[]{:S(2)}) collective-permute-start(bf16[256,64]{0,1:T(8,128)(2,1)S(1)} %get-tuple-element.23), channel_id=1, source_target_pairs={{0,2},{2,4},{4,6},{6,8},{8,10},{10,12},{12,14},{14,16},{16,18},{18... | collective-permute-start | bytes 98312 | tf_op jit(solution)/shard_map/ppermute | solution.py:13
  132.3 5.3 %collective-permute-start.9 = (bf16[256,64]{0,1:T(8,128)(2,1)S(1)}, bf16[256,64]{0,1:T(8,128)(2,1)S(1)}, u32[]{:S(2)}, u32[]{:S(2)}) collective-permute-start(bf16[256,64]{0,1:T(8,128)(2,1)S(1)} %slice.263), channel_id=1, source_target_pairs={{2,0},{4,2},{6,4},{8,6},{10,8},{12,10},{14,12},{16,14},{18,16},{20... | collective-permute-start | bytes 98312 | tf_op jit(solution)/shard_map/ppermute | solution.py:13
  138.5 3.6 %collective-permute-start.10 = (f32[64,64]{0,1:T(8,128)S(1)}, f32[64,64]{0,1:T(8,128)S(1)}, u32[]{:S(2)}, u32[]{:S(2)}) collective-permute-start(f32[64,64]{0,1:T(8,128)S(1)} %fusion.68), channel_id=1, source_target_pairs={{0,2},{2,0},{4,6},{6,4},{8,10},{10,8},{12,14},{14,12},{16,18},{18,... | collective-permute-start | bytes 49160 | tf_op jit(solution)/shard_map/ppermute | solution.py:31
  142.1 3.9 %collective-permute-start.11 = (f32[64,64]{0,1:T(8,128)S(1)}, f32[64,64]{0,1:T(8,128)S(1)}, u32[]{:S(2)}, u32[]{:S(2)}) collective-permute-start(f32[64,64]{0,1:T(8,128)S(1)} %add.177), channel_id=1, source_target_pairs={{0,4},{2,6},{4,0},{6,2},{8,12},{10,14},{12,8},{14,10},{16,20},{18,... | collective-permute-start | bytes 49160 | tf_op jit(solution)/shard_map/ppermute | solution.py:31
  146.0 3.9 %collective-permute-start.12 = (f32[64,64]{0,1:T(8,128)S(1)}, f32[64,64]{0,1:T(8,128)S(1)}, u32[]{:S(2)}, u32[]{:S(2)}) collective-permute-start(f32[64,64]{0,1:T(8,128)S(1)} %add.178), channel_id=1, source_target_pairs={{0,8},{2,10},{4,12},{6,14},{8,0},{10,2},{12,4},{14,6},{16,24},{18,... | collective-permute-start | bytes 49160 | tf_op jit(solution)/shard_map/ppermute | solution.py:31
  149.9 4.8 %collective-permute-start.13 = (f32[64,64]{0,1:T(8,128)S(1)}, f32[64,64]{0,1:T(8,128)S(1)}, u32[]{:S(2)}, u32[]{:S(2)}) collective-permute-start(f32[64,64]{0,1:T(8,128)S(1)} %add.179), channel_id=1, source_target_pairs={{0,16},{2,18},{4,20},{6,22},{8,24},{10,26},{12,28},{14,30},{16,0},... | collective-permute-start | bytes 49160 | tf_op jit(solution)/shard_map/ppermute | solution.py:31
  167.2 3.1 %collective-permute-start.14 = (bf16[256,64]{0,1:T(8,128)(2,1)S(1)}, bf16[256,64]{0,1:T(8,128)(2,1)S(1)}, u32[]{:S(2)}, u32[]{:S(2)}) collective-permute-start(bf16[256,64]{0,1:T(8,128)(2,1)S(1)} %get-tuple-element.21), channel_id=1, source_target_pairs={{0,2},{2,4},{4,6},{6,8},{8,10},{10,12},{12,14},{14,16},{16,18},{18... | collective-permute-start | bytes 98312 | tf_op jit(solution)/shard_map/ppermute | solution.py:13
  169.0 5.4 %collective-permute-start.15 = (bf16[256,64]{0,1:T(8,128)(2,1)S(1)}, bf16[256,64]{0,1:T(8,128)(2,1)S(1)}, u32[]{:S(2)}, u32[]{:S(2)}) collective-permute-start(bf16[256,64]{0,1:T(8,128)(2,1)S(1)} %slice.262), channel_id=1, source_target_pairs={{2,0},{4,2},{6,4},{8,6},{10,8},{12,10},{14,12},{16,14},{18,16},{20... | collective-permute-start | bytes 98312 | tf_op jit(solution)/shard_map/ppermute | solution.py:13
  175.2 3.6 %collective-permute-start.16 = (f32[64,64]{0,1:T(8,128)S(1)}, f32[64,64]{0,1:T(8,128)S(1)}, u32[]{:S(2)}, u32[]{:S(2)}) collective-permute-start(f32[64,64]{0,1:T(8,128)S(1)} %fusion.70), channel_id=1, source_target_pairs={{0,2},{2,0},{4,6},{6,4},{8,10},{10,8},{12,14},{14,12},{16,18},{18,... | collective-permute-start | bytes 49160 | tf_op jit(solution)/shard_map/ppermute | solution.py:31
  178.7 3.9 %collective-permute-start.17 = (f32[64,64]{0,1:T(8,128)S(1)}, f32[64,64]{0,1:T(8,128)S(1)}, u32[]{:S(2)}, u32[]{:S(2)}) collective-permute-start(f32[64,64]{0,1:T(8,128)S(1)} %add.185), channel_id=1, source_target_pairs={{0,4},{2,6},{4,0},{6,2},{8,12},{10,14},{12,8},{14,10},{16,20},{18,... | collective-permute-start | bytes 49160 | tf_op jit(solution)/shard_map/ppermute | solution.py:31
  182.7 3.9 %collective-permute-start.18 = (f32[64,64]{0,1:T(8,128)S(1)}, f32[64,64]{0,1:T(8,128)S(1)}, u32[]{:S(2)}, u32[]{:S(2)}) collective-permute-start(f32[64,64]{0,1:T(8,128)S(1)} %add.186), channel_id=1, source_target_pairs={{0,8},{2,10},{4,12},{6,14},{8,0},{10,2},{12,4},{14,6},{16,24},{18,... | collective-permute-start | bytes 49160 | tf_op jit(solution)/shard_map/ppermute | solution.py:31
  186.6 4.8 %collective-permute-start.19 = (f32[64,64]{0,1:T(8,128)S(1)}, f32[64,64]{0,1:T(8,128)S(1)}, u32[]{:S(2)}, u32[]{:S(2)}) collective-permute-start(f32[64,64]{0,1:T(8,128)S(1)} %add.187), channel_id=1, source_target_pairs={{0,16},{2,18},{4,20},{6,22},{8,24},{10,26},{12,28},{14,30},{16,0},... | collective-permute-start | bytes 49160 | tf_op jit(solution)/shard_map/ppermute | solution.py:31
  (4 other events, 26.8 us)
